TPU v7x, 32 devices: a whole 2x2x4 slice. The times are simulated.
32 devices in a mesh: dp: 2 (over x), row: 4 (over y, core), col: 4 (over z).
Axes of the slice: x: 2, y: 2, z: 4, core: 2. Of those that a mesh axis runs over, the one named last changes fastest.
Arguments:
- inputs: bfloat16 [4096, 2048], P(('dp', 'row'), 'col'), may hold values from -6 to 6
- cotangent: bfloat16 [4096, 2048], P(('dp', 'row'), 'col'), may hold values from -6 to 6
- segments: int32 [4096], P('dp'), may hold values from 1999 to 4095, as said below
- positions: int32 [4096], P('dp'), may hold values from 0 to 1999, as said below
- w_qkv: bfloat16 [2048, 3, 2048], P('col', None, 'row'), may hold values from -1 to 1
- w_out: bfloat16 [2048, 2048], P('row', 'col'), may hold values from -0.5 to 0.5
- w_up: bfloat16 [2048, 8192], P('col', 'row'), may hold values from -1 to 1
- w_down: bfloat16 [8192, 2048], P('row', 'col'), may hold values from -0.0625 to 0.0625
- vectors: float32 [11, 2048], replicated, may hold values from -1.5 to 3
- tile_moment: float32 [4, 4, 24, 512, 256], P('row', 'col', 'dp'), may hold values from -40 to 40
- vector_moment: float32 [11, 2048], replicated, may hold values from -3 to 3
Outputs:
- result: float32 [4096, 2048], P(('dp', 'row'), 'col')
- grad_input: float32 [4096, 2048], P(('dp', 'row'), 'col')
- tile_grads: float32 [4, 4, 24, 512, 256], P('row', 'col', 'dp')
- new_tiles: float32 [4, 4, 24, 512, 256], P('row', 'col', 'dp')
- new_tile_moment: float32 [4, 4, 24, 512, 256], P('row', 'col', 'dp')
- vector_grads: float32 [11, 2048], replicated
- new_vectors: float32 [11, 2048], replicated
- new_vector_moment: float32 [11, 2048], replicated
Inputs may be any that keep to these rules, and one draw needn't show every extreme that they name: `segments`: each token's document label, the index in the whole array of its document's last token (the last document's label is 4095); labels never fall; every document but the last has 200 to 2000 tokens, documents run on across sequence ends, and the first has exactly 2000. `positions`: each token's place in its document, counted from 0 and running on across sequence ends.
All inputs are finite; a program needn't handle non-finite values.
Results may differ from a plain program's by a relative error of at most 0.015.
The roundings to bfloat16 on the way count: a program that leaves them out, or rounds other values in their place, can miss the bound.
Values may be sent and summed in bfloat16 or wider, within the bound.
A program may use at most 256 MiB of HBM per device.

v0:
```python
import math
import jax
import jax.numpy as jnp
from jax import lax
from jax.sharding import PartitionSpec as P

HEAD_DIM = 64
ROTARY = 32
SEQ_LEN = 512
MOMENTUM_RATE = 0.95
MUON_RATE = 0.05
VECTOR_RATE = 0.12
NEWTON_A = 3.4445
NEWTON_B = -4.775
NEWTON_C = 2.0315
GELU_SCALE = 0.7978845608028654
GELU_CUBIC = 0.044715
NORM_EPS = 1e-05
STAT_EPS = 1e-06
MASKED_SCORE = -1e30


def to_low(tensor_in):
    return lax.optimization_barrier(tensor_in.astype(jnp.bfloat16))


def gelu_value(pre_act):
    inner_arg = GELU_SCALE * (pre_act + GELU_CUBIC * pre_act * pre_act * pre_act)
    return 0.5 * pre_act * (1.0 + jnp.tanh(inner_arg))


def gelu_slope(pre_act):
    tanh_val = jnp.tanh(GELU_SCALE * (pre_act + GELU_CUBIC * pre_act * pre_act * pre_act))
    return 0.5 * (1.0 + tanh_val) + 0.5 * pre_act * (1.0 - tanh_val * tanh_val) * GELU_SCALE * (
        1.0 + 3.0 * GELU_CUBIC * pre_act * pre_act
    )


def rotary_tables(positions):
    half_dims = ROTARY // 2
    frequency = jnp.exp(
        jnp.arange(half_dims, dtype=jnp.float32) * (-2.0 * math.log(10000.0) / ROTARY)
    )
    angles = positions.astype(jnp.float32)[:, None] * frequency[None, :]
    return (jnp.cos(angles), jnp.sin(angles))


def rotate(tensor_in, cosine, sine_tab, direction_sign):
    half_dims = ROTARY // 2
    first_half = tensor_in[..., :half_dims]
    second_half = tensor_in[..., half_dims:ROTARY]
    cos_wide = cosine[:, None, :]
    sin_wide = sine_tab[:, None, :] * direction_sign
    return jnp.concatenate(
        [
            first_half * cos_wide - second_half * sin_wide,
            second_half * cos_wide + first_half * sin_wide,
            tensor_in[..., ROTARY:],
        ],
        axis=-1,
    )


def causal_allowed(segment):
    token_order = jnp.arange(segment.shape[0])
    return (segment[:, None] == segment[None, :]) & (token_order[:, None] >= token_order[None, :])


def masked_scores(queries, key_vecs, segment, score_scale):
    scores = (
        jnp.einsum("lhe,mhe->hlm", queries, key_vecs, preferred_element_type=jnp.float32)
        * score_scale
    )
    return jnp.where(causal_allowed(segment)[None], scores, MASKED_SCORE)


def attend_forward(queries, key_vecs, values, segment, score_scale):
    scores = masked_scores(queries, key_vecs, segment, score_scale)
    row_max = jnp.max(scores, axis=-1, keepdims=True)
    exp_scores = jnp.exp(scores - row_max)
    row_total = jnp.sum(exp_scores, axis=-1, keepdims=True)
    probs_low = to_low(exp_scores / row_total)
    attended = jnp.einsum("hlm,mhe->lhe", probs_low, values, preferred_element_type=jnp.float32)
    return (attended, (row_max + jnp.log(row_total))[..., 0])


def attend_backward(queries, key_vecs, values, output_low, grad_low, logsum, segment, score_scale):
    scores = masked_scores(queries, key_vecs, segment, score_scale)
    probs = jnp.exp(scores - logsum[..., None])
    grad_values = jnp.einsum(
        "hlm,lhe->mhe", to_low(probs), grad_low, preferred_element_type=jnp.float32
    )
    grad_probs = jnp.einsum("lhe,mhe->hlm", grad_low, values, preferred_element_type=jnp.float32)
    row_delta = jnp.sum(grad_low.astype(jnp.float32) * output_low.astype(jnp.float32), axis=-1)
    grad_scores = to_low(probs * (grad_probs - row_delta.T[:, :, None]) * score_scale)
    grad_queries = jnp.einsum(
        "hlm,mhe->lhe", grad_scores, key_vecs, preferred_element_type=jnp.float32
    )
    grad_keys = jnp.einsum("hlm,lhe->mhe", grad_scores, queries, preferred_element_type=jnp.float32)
    return (grad_queries, grad_keys, grad_values)


def newton_schulz(moment):
    iterate = to_low(moment * lax.rsqrt(jnp.sum(moment * moment) + STAT_EPS))
    for newton_step in range(5):
        gram = to_low(jnp.dot(iterate.T, iterate, preferred_element_type=jnp.float32))
        square = jnp.dot(gram, gram, preferred_element_type=jnp.float32)
        poly = to_low(NEWTON_B * gram.astype(jnp.float32) + NEWTON_C * square)
        iterate = to_low(
            NEWTON_A * iterate.astype(jnp.float32)
            + jnp.dot(iterate, poly, preferred_element_type=jnp.float32)
        )
    return iterate


def tile_blocks(qkv_block, out_block, up_block, down_block):
    tile_rows = qkv_block.shape[0]
    tile_cols = qkv_block.shape[2] // 2

    def split_cols(block_in):
        return block_in.reshape(
            block_in.shape[0], block_in.shape[1] // tile_cols, tile_cols
        ).transpose(1, 0, 2)

    down_part = down_block.reshape(
        down_block.shape[0] // tile_rows, tile_rows, down_block.shape[1] // tile_cols, tile_cols
    )
    down_part = down_part.transpose(0, 2, 1, 3).reshape(-1, tile_rows, tile_cols)
    return jnp.concatenate(
        [
            split_cols(qkv_block[:, 0]),
            split_cols(qkv_block[:, 1]),
            split_cols(qkv_block[:, 2]),
            split_cols(out_block),
            split_cols(up_block),
            down_part,
        ],
        axis=0,
    )


def body(
    inputs,
    cotangent,
    segments,
    positions,
    w_qkv,
    w_out,
    w_up,
    w_down,
    vectors,
    tile_moment,
    vector_moment,
):
    row_index = lax.axis_index("row")
    col_index = lax.axis_index("col")
    col_count = lax.axis_size("col")
    row_count_axis = lax.axis_size("row")
    local_rows, col_width = inputs.shape
    model_width = vectors.shape[1]
    row_width = w_qkv.shape[2]
    head_feats = row_width // col_count
    unit_width = w_up.shape[1] // col_count
    up_total = w_up.shape[1] * row_count_axis
    score_scale = HEAD_DIM ** (-0.5)
    feat_start = (row_index * col_count + col_index) * head_feats
    unit_start = (row_index * col_count + col_index) * unit_width
    col_start = col_index * col_width
    norm_gain = lax.dynamic_slice_in_dim(vectors[5], col_start, col_width)
    norm_shift = lax.dynamic_slice_in_dim(vectors[6], col_start, col_width)
    out_bias = lax.dynamic_slice_in_dim(vectors[3] + vectors[4], col_start, col_width)
    qkv_bias = lax.dynamic_slice_in_dim(vectors[0:3], feat_start, head_feats, axis=1)
    up_bias = lax.dynamic_slice_in_dim(vectors[7:].reshape(-1), unit_start, unit_width)
    x_val = inputs.astype(jnp.float32)
    row_stats = lax.psum((jnp.sum(x_val, axis=1), jnp.sum(x_val * x_val, axis=1)), "col")
    mean_x = (row_stats[0] / model_width)[:, None]
    var_x = (row_stats[1] / model_width)[:, None] - mean_x * mean_x
    inv_std = lax.rsqrt(var_x + NORM_EPS)
    x_hat = (x_val - mean_x) * inv_std
    normed = (x_hat * norm_gain + norm_shift).astype(jnp.bfloat16)
    gathered, cot_rows = (
        lax.all_gather(normed, "row", axis=0, tiled=True),
        lax.all_gather(cotangent, "row", axis=0, tiled=True),
    )
    seq_rows = gathered.shape[0]
    qkv_perm = (
        w_qkv.reshape(col_width, 3, col_count, head_feats)
        .transpose(0, 2, 1, 3)
        .reshape(col_width, col_count, 3 * head_feats)
    )
    w_in = jnp.concatenate([qkv_perm, w_up.reshape(col_width, col_count, unit_width)], axis=2)
    group_width = w_in.shape[2]
    w_in_flat = w_in.reshape(col_width, col_count * group_width)
    mixed_out = lax.psum_scatter(
        jnp.dot(gathered, w_in_flat, preferred_element_type=jnp.float32),
        "col",
        scatter_dimension=1,
        tiled=True,
    )
    qkv_part = mixed_out[:, : 3 * head_feats].reshape(seq_rows, 3, head_feats) + qkv_bias[None]
    up_pre = mixed_out[:, 3 * head_feats :] + up_bias
    heads_here = head_feats // HEAD_DIM
    seq_count = seq_rows // SEQ_LEN

    def by_seq(tensor_in):
        return tensor_in.reshape((seq_count, SEQ_LEN) + tensor_in.shape[1:])

    cosine, sine_tab = rotary_tables(positions)
    queries = rotate(
        qkv_part[:, 0].reshape(seq_rows, heads_here, HEAD_DIM), cosine, sine_tab, 1.0
    ).astype(jnp.bfloat16)
    key_vecs = rotate(
        qkv_part[:, 1].reshape(seq_rows, heads_here, HEAD_DIM), cosine, sine_tab, 1.0
    ).astype(jnp.bfloat16)
    values = qkv_part[:, 2].reshape(seq_rows, heads_here, HEAD_DIM).astype(jnp.bfloat16)
    attended, logsum = jax.vmap(attend_forward, in_axes=(0, 0, 0, 0, None))(
        by_seq(queries), by_seq(key_vecs), by_seq(values), by_seq(segments), score_scale
    )
    attn_low = attended.reshape(seq_rows, head_feats).astype(jnp.bfloat16)
    act_low = gelu_value(up_pre).astype(jnp.bfloat16)
    attn_rows, act_rows = (
        lax.all_gather(attn_low, "col", axis=1, tiled=True),
        lax.all_gather(act_low, "col", axis=1, tiled=True),
    )
    branch = lax.psum_scatter(
        jnp.dot(attn_rows, w_out, preferred_element_type=jnp.float32)
        + jnp.dot(act_rows, w_down, preferred_element_type=jnp.float32),
        "row",
        scatter_dimension=0,
        tiled=True,
    )
    result = x_val + branch + out_bias
    cot_val = cotangent.astype(jnp.float32)
    grad_w_out = jnp.einsum("ti,tj->ij", attn_rows, cot_rows, preferred_element_type=jnp.float32)
    grad_w_down = jnp.einsum("ti,tj->ij", act_rows, cot_rows, preferred_element_type=jnp.float32)
    back_attn = jnp.einsum("tj,ij->ti", cot_rows, w_out, preferred_element_type=jnp.float32)
    back_act = jnp.einsum("tj,ij->ti", cot_rows, w_down, preferred_element_type=jnp.float32)
    grad_attn, grad_act = (
        lax.psum_scatter(back_attn, "col", scatter_dimension=1, tiled=True),
        lax.psum_scatter(back_act, "col", scatter_dimension=1, tiled=True),
    )
    grad_attn_low = grad_attn.astype(jnp.bfloat16)
    grad_up = grad_act * gelu_slope(up_pre)
    g_queries, g_keys, g_values = jax.vmap(attend_backward, in_axes=(0, 0, 0, 0, 0, 0, 0, None))(
        by_seq(queries),
        by_seq(key_vecs),
        by_seq(values),
        by_seq(attn_low.reshape(seq_rows, heads_here, HEAD_DIM)),
        by_seq(grad_attn_low.reshape(seq_rows, heads_here, HEAD_DIM)),
        logsum,
        by_seq(segments),
        score_scale,
    )
    g_queries = rotate(
        g_queries.reshape(seq_rows, heads_here, HEAD_DIM), cosine, sine_tab, -1.0
    ).reshape(seq_rows, head_feats)
    g_keys = rotate(g_keys.reshape(seq_rows, heads_here, HEAD_DIM), cosine, sine_tab, -1.0).reshape(
        seq_rows, head_feats
    )
    g_values = g_values.reshape(seq_rows, head_feats)
    grad_mixed = jnp.concatenate([g_queries, g_keys, g_values, grad_up], axis=1)
    grad_cols = lax.all_gather(grad_mixed.astype(jnp.bfloat16), "col", axis=1, tiled=True)
    grad_w_in = jnp.einsum("ti,tj->ij", gathered, grad_cols, preferred_element_type=jnp.float32)
    grad_norm = lax.psum_scatter(
        jnp.einsum("tj,ij->ti", grad_cols, w_in_flat, preferred_element_type=jnp.float32),
        "row",
        scatter_dimension=0,
        tiled=True,
    )
    grad_hat = grad_norm * norm_gain
    back_stats = lax.psum((jnp.sum(grad_hat, axis=1), jnp.sum(grad_hat * x_hat, axis=1)), "col")
    grad_x = inv_std * (
        grad_hat
        - (back_stats[0] / model_width)[:, None]
        - x_hat * (back_stats[1] / model_width)[:, None]
    )
    grad_input = cot_val + grad_x
    qkv_sums = jnp.sum(grad_mixed[:, : 3 * head_feats].reshape(seq_rows, 3, head_feats), axis=0)
    out_sums = jnp.sum(cot_val, axis=0)
    norm_sums = jnp.stack(
        [out_sums, out_sums, jnp.sum(grad_norm * x_hat, axis=0), jnp.sum(grad_norm, axis=0)]
    )
    qkv_rows = lax.dynamic_update_slice_in_dim(
        jnp.zeros((3, model_width), jnp.float32), qkv_sums, feat_start, axis=1
    )
    norm_rows = lax.dynamic_update_slice_in_dim(
        jnp.zeros((4, model_width), jnp.float32), norm_sums, col_start, axis=1
    )
    up_rows = lax.dynamic_update_slice_in_dim(
        jnp.zeros((up_total,), jnp.float32), jnp.sum(grad_up, axis=0), unit_start, axis=0
    ).reshape(-1, model_width)
    local_vec = jnp.concatenate([qkv_rows, norm_rows, up_rows], axis=0)
    vec_grad = lax.psum(local_vec, ("dp", "row", "col"))
    scaled = vec_grad * lax.rsqrt(jnp.mean(vec_grad * vec_grad, axis=1, keepdims=True) + STAT_EPS)
    vec_moment_new = MOMENTUM_RATE * vector_moment + scaled
    vectors_new = vectors - VECTOR_RATE * vec_moment_new
    grad_perm = grad_w_in.reshape(col_width, col_count, group_width)
    grad_qkv = (
        grad_perm[:, :, : 3 * head_feats]
        .reshape(col_width, col_count, 3, head_feats)
        .transpose(0, 2, 1, 3)
        .reshape(col_width, 3, row_width)
    )
    grad_up_w = grad_perm[:, :, 3 * head_feats :].reshape(col_width, col_count * unit_width)
    grad_tiles = tile_blocks(grad_qkv, grad_w_out, grad_up_w, grad_w_down)
    owned_grads = lax.psum_scatter(grad_tiles[None, None], "dp", scatter_dimension=2, tiled=True)
    owned_count = owned_grads.shape[2]
    weight_tiles = lax.dynamic_slice_in_dim(
        tile_blocks(w_qkv, w_out, w_up, w_down), lax.axis_index("dp") * owned_count, owned_count, 0
    ).astype(jnp.float32)
    moment_new = MOMENTUM_RATE * tile_moment[0, 0] + owned_grads[0, 0]
    ortho_tiles = jax.vmap(newton_schulz)(moment_new)
    tile_ratio = math.sqrt(max(1.0, moment_new.shape[1] / moment_new.shape[2]))
    tiles_new = weight_tiles - MUON_RATE * tile_ratio * ortho_tiles.astype(jnp.float32)
    return (
        result,
        grad_input,
        owned_grads,
        tiles_new[None, None],
        moment_new[None, None],
        vec_grad,
        vectors_new,
        vec_moment_new,
    )


def solution(mesh):
    placed = (
        P(("dp", "row"), "col"),
        P(("dp", "row"), "col"),
        P("dp"),
        P("dp"),
        P("col", None, "row"),
        P("row", "col"),
        P("col", "row"),
        P("row", "col"),
        P(),
        P("row", "col", "dp", None, None),
        P(),
    )
    return jax.shard_map(
        body,
        mesh=mesh,
        in_specs=placed,
        out_specs=(
            P(("dp", "row"), "col"),
            P(("dp", "row"), "col"),
            P("row", "col", "dp", None, None),
            P("row", "col", "dp", None, None),
            P("row", "col", "dp", None, None),
            P(),
            P(),
            P(),
        ),
        check_vma=False,
    )
```

profile of v0, /device:TPU:0, one launch (start us, length us, event | category | flops | bytes accessed | tf_op | source)
XLA Modules:
  0.0 1773.4 jit_solution(18095130869114446671)
XLA Ops:
  9.2 13.5 all-reduce.1
  24.4 2.1 fusion.18
  26.5 8.3 all-gather.12.cloned.1.call-done
  34.9 5.0 fusion.35
  41.4 2.7 reshape.239
  47.6 3.0 copy.86
  50.6 3.2 pad_maximum_fusion
  53.9 2.4 copy.158
  56.3 3.3 all-gather.6.cloned.1.call-done
  59.6 16.2 fusion.33
  77.4 9.7 fusion.36
  91.7 47.6 %reduce-scatter.11.cloned.1.call-done = f32[2048,128]{1,0:T(8,128)} async-done(((f32[2048,512]{1,0:T(8,128)}), f32[2048,128]{1,0:T(8,128)}) %reduce-scatter.11.cloned.1.call-update) | async-done | bytes 1048592 | tf_op jit(solution)/shard_map/reduce_scatter | solution.py:239
  142.8 480.9 %reduce-scatter.7.cloned.1.call-done = f32[2048,896]{1,0:T(8,128)} async-done(((f32[2048,3584]{1,0:T(8,128)}), f32[2048,896]{1,0:T(8,128)}) %reduce-scatter.7.cloned.1.call-update) | async-done | bytes 7340048 | tf_op jit(solution)/shard_map/reduce_scatter | solution.py:194
  623.7 3.8 slice.129
  627.5 2.4 copy.87
  636.7 4.5 fusion.1
  645.8 4.0 multiply_reduce_fusion
  649.8 6.1 multiply_convert_fusion
  663.4 245.1 %reduce-scatter.13.cloned.1.call-done = f32[2048,512]{1,0:T(8,128)} async-done(((f32[2048,2048]{1,0:T(8,128)}), f32[2048,512]{1,0:T(8,128)}) %reduce-scatter.13.cloned.1.call-update) | async-done | bytes 4194320 | tf_op jit(solution)/shard_map/reduce_scatter | solution.py:240
  908.5 6.5 fusion.27
  915.1 2.1 pad_maximum_fusion.1
  920.4 250.0 %all-gather.14.cloned.1.call-done = bf16[2048,3584]{1,0:T(8,128)(2,1)} async-done(((bf16[2048,896]{1,0:T(8,128)(2,1)}), bf16[2048,3584]{1,0:T(8,128)(2,1)}) %all-gather.14.cloned.1.call-update) | async-done | bytes 14680080 | tf_op jit(solution)/shard_map/all_gather | solution.py:262
  1170.4 13.4 fusion.37
  1183.9 136.5 %all-gather.10.cloned.1.call-done = bf16[2048,2048]{1,0:T(8,128)(2,1)} async-done(((bf16[2048,512]{1,0:T(8,128)(2,1)}), bf16[2048,2048]{1,0:T(8,128)(2,1)}) %all-gather.10.cloned.1.call-update) | async-done | bytes 8388624 | tf_op jit(solution)/shard_map/all_gather | solution.py:223
  1320.3 10.5 fusion.34
  1330.9 35.5 %all-gather.8.cloned.1.call-done = bf16[2048,512]{0,1:T(8,128)(2,1)} async-done(((bf16[2048,128]{0,1:T(8,128)(2,1)}), bf16[2048,512]{0,1:T(8,128)(2,1)}) %all-gather.8.cloned.1.call-update) | async-done | bytes 2097168 | tf_op jit(solution)/shard_map/all_gather | solution.py:222
  1366.4 6.3 convolution_add_fusion
  1373.5 4.7 fusion.39
  1379.9 9.7 fusion.40
  1389.6 5.9 reshape.252
  1395.5 4.8 copy.120
  1400.2 11.4 fusion.38
  1412.0 2.5 slice.150
  1418.3 2.5 copy.116
  1420.9 5.7 copy.119
  1430.8 2.5 bitcast_dynamic-update-slice_fusion
  1435.2 9.7 all-reduce
  1444.9 15.5 reduce-scatter.9.cloned.1.call-done
  1460.5 3.3 convert_reduce_fusion.1
  1464.6 4.5 constant_dynamic-update-slice_fusion
  1471.2 4.0 copy.129
  1475.2 4.0 reshape.256
  1481.7 2.1 copy.124
  1486.0 2.6 copy.130
  1498.9 92.2 %all-reduce.4.cloned.1.call-done = f32[11,2048]{1,0:T(8,128)} async-done(((f32[11,2048]{1,0:T(8,128)}), f32[11,2048]{1,0:T(8,128)}) %all-reduce.4.cloned.1.call-update) | async-done | bytes 90128 | tf_op jit(solution)/shard_map/psum | solution.py:293
  1593.9 143.6 %reduce-scatter.17.cloned.1.call-done = f32[1,1,12,512,256]{4,3,2,1,0:T(8,128)} async-done(((f32[1,1,24,512,256]{4,3,2,1,0:T(8,128)}), f32[1,1,12,512,256]{4,3,2,1,0:T(8,128)}) %reduce-scatter.17.cloned.1.call-update) | async-done | bytes 6291472 | tf_op jit(solution)/shard_map/reduce_scatter | solution.py:306
  1737.4 5.7 fusion.2
  1759.9 5.5 subtract_bitcast_fusion
  (213 shorter events, 91.0 us)
Async XLA Ops:
  7.2 27.7 %all-gather.12.cloned.1.call-start = ((), (), s32[]{:S(2)}) async-start(), calls=%async_computation.11 | async-start | bytes 2621440 | tf_op jit(solution)/shard_map/all_gather | solution.py:183
  7.9 51.7 %all-gather.6.cloned.1.call-start = ((), (), s32[]{:S(2)}) async-start(), calls=%async_computation.6 | async-start | bytes 2621440 | tf_op jit(solution)/shard_map/all_gather | solution.py:182
  26.5 112.8 %reduce-scatter.11.cloned.1.call-start = ((), (), s32[]{:S(2)}) async-start(), calls=%async_computation.12 | async-start | bytes 5242880 | tf_op jit(solution)/shard_map/reduce_scatter | solution.py:239
  39.8 1.6 copy-start.6
  39.9 583.9 %reduce-scatter.7.cloned.1.call-start = ((), (), s32[]{:S(2)}) async-start(), calls=%async_computation.7 | async-start | bytes 36700160 | tf_op jit(solution)/shard_map/reduce_scatter | solution.py:194
  46.1 7.7 copy-start.3
  75.8 1.6 copy-start.10
  75.8 832.7 %reduce-scatter.13.cloned.1.call-start = ((), (), s32[]{:S(2)}) async-start(), calls=%async_computation.13 | async-start | bytes 20971520 | tf_op jit(solution)/shard_map/reduce_scatter | solution.py:240
  87.1 0.9 copy-start.36
  87.1 1.0 copy-start.37
  87.1 1.6 slice-start
  87.1 1083.3 %all-gather.14.cloned.1.call-start = ((), (), s32[]{:S(2)}) async-start(), calls=%async_computation.14 | async-start | bytes 18350080 | tf_op jit(solution)/shard_map/all_gather | solution.py:262
  630.2 1.2 copy-start.5
  630.7 2.6 copy-start.23
  631.4 1.9 copy-start.21
  633.3 3.4 copy-start
  636.7 4.5 copy-start.13
  645.8 4.1 copy-start.19
  649.8 6.1 copy-start.24
  655.9 1.5 copy-start.22
  657.5 1.8 copy-start.25
  660.1 248.4 %copy-start.35 = (f32[512]{0:T(512)S(1)}, f32[512]{0:T(512)}, u32[]{:S(2)}) copy-start(f32[512]{0:T(512)} %dynamic_slice.23) | copy-start | bytes 6148
  908.5 6.5 copy-start.15
  908.5 6.5 copy-start.16
  908.5 6.5 copy-start.17
  917.1 403.2 %all-gather.10.cloned.1.call-start = ((), (), s32[]{:S(2)}) async-start(), calls=%async_computation.9 | async-start | bytes 10485760 | tf_op jit(solution)/shard_map/all_gather | solution.py:223
  917.9 448.5 %all-gather.8.cloned.1.call-start = ((), (), s32[]{:S(2)}) async-start(), calls=%async_computation.8 | async-start | bytes 2621440 | tf_op jit(solution)/shard_map/all_gather | solution.py:222
  920.3 513.0 %reduce-scatter.15.cloned.1.call-start = ((), (), s32[]{:S(2)}) async-start(), calls=%async_computation.15 | async-start | bytes 5242880 | tf_op jit(solution)/shard_map/reduce_scatter | solution.py:264
  1183.8 276.6 %reduce-scatter.9.cloned.1.call-start = ((), (), s32[]{:S(2)}) async-start(), calls=%async_computation.10 | async-start | bytes 5242880 | tf_op jit(solution)/shard_map/reduce_scatter | solution.py:225
  1372.7 218.4 %all-reduce.4.cloned.1.call-start = ((), (), s32[]{:S(2)}) async-start(), calls=%async_computation.17 | async-start | bytes 262144 | tf_op jit(solution)/shard_map/psum | solution.py:293
  1373.5 6.4 copy-start.11
  1395.5 4.8 copy-start.38
  1426.5 2.1 copy-start.14
  1427.6 3.1 copy-start.2
  1430.8 2.5 copy-start.9
  1430.8 2.5 copy-start.30
  1430.8 2.5 copy-start.32
  1430.8 2.5 copy-start.34
  1430.8 29.7 %copy-start.18 = (bf16[512,512]{1,0:T(8,128)(2,1)S(1)}, bf16[512,512]{1,0:T(8,128)(2,1)}, u32[]{:S(2)}) copy-start(bf16[512,512]{1,0:T(8,128)(2,1)} %param.12) | copy-start | bytes 1572868
  1464.5 272.9 %reduce-scatter.17.cloned.1.call-start = ((), (), s32[]{:S(2)}) async-start(), calls=%async_computation.16 | async-start | bytes 18874368 | tf_op jit(solution)/shard_map/reduce_scatter | solution.py:306
  1469.1 1.0 copy-start.12
  1471.2 8.0 copy-start.4
  1480.3 5.7 copy-start.8
  1490.5 5.5 copy-start.7
  1496.0 96.2 %copy-start.27 = (f32[11,2048]{1,0:T(8,128)S(1)}, f32[11,2048]{1,0:T(8,128)}, u32[]{:S(2)}) copy-start(f32[11,2048]{1,0:T(8,128)} %param.19) | copy-start | bytes 270340
  1496.0 96.2 %copy-start.28 = (f32[11,2048]{1,0:T(8,128)S(1)}, f32[11,2048]{1,0:T(8,128)}, u32[]{:S(2)}) copy-start(f32[11,2048]{1,0:T(8,128)} %param.21) | copy-start | bytes 270340
  1743.1 2.7 copy-start.1
  1759.9 5.6 copy-start.20
  (4 other events, 2.6 us)
Sparse Core Ops, SparseCore 0:
  9.5 25.2 all-gather.11
  37.0 22.5 all-gather.5
  62.5 76.7 reduce-scatter.10
  141.5 482.1 reduce-scatter.6
  625.9 282.5 reduce-scatter.12
  917.3 253.0 all-gather.13
  1172.5 147.7 all-gather.9
  1322.5 43.8 all-gather.7
  1369.5 43.3 reduce-scatter.14
  1415.8 44.5 reduce-scatter.8
  1466.6 124.5 all-reduce.3
  1593.8 143.5 reduce-scatter.16
where the time goes:
time: 1780 us; the launch traced here: 1770 us
  waiting for transfers between devices  1460 us (82%)
  matrix products  116 us (7%)
  local copies, waits for them, and re-layouts  108 us (6%)
  other arithmetic  49.4 us (3%)
  blocking collectives  23.1 us (1%)
    reduce_scatter x1, waiting for transfers between devices, body(): lax.psum_scatter(jnp.dot(gathered, w_in_flat, preferred_element_type=jnp....  481 us
    all_gather x1, waiting for transfers between devices, body(): lax.all_gather(grad_mixed.astype(jnp.bfloat16), 'col', axis=1, tiled=True)  250 us
    reduce_scatter x1, waiting for transfers between devices, body(): lax.psum_scatter(back_act, 'col', scatter_dimension=1, tiled=True)  245 us
    reduce_scatter x1, waiting for transfers between devices, body(): lax.psum_scatter(grad_tiles[None, None], 'dp', scatter_dimension=2, tiled...  144 us
    all_gather x1, waiting for transfers between devices, body(): lax.all_gather(act_low, 'col', axis=1, tiled=True)  136 us
    psum x1, waiting for transfers between devices, body(): vec_grad = lax.psum(local_vec, ('dp', 'row', 'col'))  92.2 us
    reduce_scatter x1, waiting for transfers between devices, body(): lax.psum_scatter(back_attn, 'col', scatter_dimension=1, tiled=True)  47.6 us
  transfers between devices with their start and end apart: 12, of which 11 were waited for; matrix products, arithmetic and copies ran while one was open for 13% of the time, Pallas kernels for 0%

commit v1 on v0

--- a/solution.py
+++ b/solution.py
@@ -290,7 +290,10 @@
         jnp.zeros((up_total,), jnp.float32), jnp.sum(grad_up, axis=0), unit_start, axis=0
     ).reshape(-1, model_width)
     local_vec = jnp.concatenate([qkv_rows, norm_rows, up_rows], axis=0)
-    vec_grad = lax.psum(local_vec, ("dp", "row", "col"))
+    supply_all_stages_all_by_axis = lambda arr_in, mesh_name: jnp.sum(
+        lax.all_gather(arr_in, mesh_name), axis=0
+    )
+    vec_grad = supply_all_stages_all_by_axis(local_vec, ("dp", "row", "col"))
     scaled = vec_grad * lax.rsqrt(jnp.mean(vec_grad * vec_grad, axis=1, keepdims=True) + STAT_EPS)
     vec_moment_new = MOMENTUM_RATE * vector_moment + scaled
     vectors_new = vectors - VECTOR_RATE * vec_moment_new

time: 1780 us -> 1720 us (0.966)
  waiting for transfers between devices: 1460 us -> 1400 us
    psum x1 -> x0, waiting for transfers between devices: 92.2 us -> none  [body(): vec_grad = lax.psum(local_vec, ('dp', 'row', 'col'))]
    reduce_scatter x1, waiting for transfers between devices: 0.01 us -> 33.8 us  [body(): lax.psum_scatter(jnp.einsum('tj,ij->ti', grad_cols, w_in_flat, preferred_...]
    reduce_scatter x1, waiting for transfers between devices: 144 us -> 121 us  [body(): lax.psum_scatter(grad_tiles[None, None], 'dp', scatter_dimension=2, tiled...]
    reduce_scatter x1, waiting for transfers between devices: 15.5 us -> 34.1 us  [body(): lax.psum_scatter(jnp.dot(attn_rows, w_out, preferred_element_type=jnp.flo...]
    unnamed x101 -> x90, local copies, waits for them, and re-layouts: 34.4 us -> 35.7 us
  transfers between devices with their start and end apart: 12 -> 12, of which waited for: 11 -> 11; matrix products, arithmetic and copies ran while one was open for 13% -> 12% of each run, Pallas kernels for 0% -> 0%
where the time goes in v1:
time: 1720 us; the launch traced here: 1710 us
  waiting for transfers between devices  1400 us (81%)
  matrix products  115 us (7%)
  local copies, waits for them, and re-layouts  102 us (6%)
  other arithmetic  50.6 us (3%)
  blocking collectives  25.2 us (1%)
    reduce_scatter x1, waiting for transfers between devices, body(): lax.psum_scatter(jnp.dot(gathered, w_in_flat, preferred_element_type=jnp....  481 us
    all_gather x1, waiting for transfers between devices, body(): lax.all_gather(grad_mixed.astype(jnp.bfloat16), 'col', axis=1, tiled=True)  250 us
    reduce_scatter x1, waiting for transfers between devices, body(): lax.psum_scatter(back_act, 'col', scatter_dimension=1, tiled=True)  245 us
    all_gather x1, waiting for transfers between devices, body(): lax.all_gather(act_low, 'col', axis=1, tiled=True)  136 us
    reduce_scatter x1, waiting for transfers between devices, body(): lax.psum_scatter(grad_tiles[None, None], 'dp', scatter_dimension=2, tiled...  121 us
    reduce_scatter x1, waiting for transfers between devices, body(): lax.psum_scatter(back_attn, 'col', scatter_dimension=1, tiled=True)  48.1 us
    unnamed x90, local copies, waits for them, and re-layouts  35.7 us
    all_gather x1, waiting for transfers between devices, body(): lax.all_gather(attn_low, 'col', axis=1, tiled=True)  35.5 us
  transfers between devices with their start and end apart: 12, of which 11 were waited for; matrix products, arithmetic and copies ran while one was open for 12% of the time, Pallas kernels for 0%

profile of v1, /device:TPU:0, one launch (start us, length us, event | category | flops | bytes accessed | tf_op | source)
XLA Modules:
  0.0 1707.6 jit_solution(17378439827062314961)
XLA Ops:
  9.2 13.5 all-reduce.1
  24.4 2.1 fusion.18
  26.5 8.3 all-gather.15.cloned.1.call-done
  34.9 5.0 fusion.35
  41.4 2.7 reshape.239
  47.6 3.0 copy.139
  50.6 3.2 pad_maximum_fusion
  53.9 2.4 copy.211
  56.3 3.3 all-gather.9.cloned.1.call-done
  59.6 16.2 fusion.33
  77.4 9.7 fusion.36
  91.1 48.1 %reduce-scatter.11.cloned.1.call-done = f32[2048,128]{1,0:T(8,128)} async-done(((f32[2048,512]{1,0:T(8,128)}), f32[2048,128]{1,0:T(8,128)}) %reduce-scatter.11.cloned.1.call-update) | async-done | bytes 1048592 | tf_op jit(solution)/shard_map/reduce_scatter | solution.py:239
  142.8 480.9 %reduce-scatter.7.cloned.1.call-done = f32[2048,896]{1,0:T(8,128)} async-done(((f32[2048,3584]{1,0:T(8,128)}), f32[2048,896]{1,0:T(8,128)}) %reduce-scatter.7.cloned.1.call-update) | async-done | bytes 7340048 | tf_op jit(solution)/shard_map/reduce_scatter | solution.py:194
  623.7 3.8 slice.129
  627.5 2.4 copy.140
  633.4 2.0 fusion
  636.7 4.5 fusion.1
  645.8 4.0 multiply_reduce_fusion
  649.8 6.0 multiply_convert_fusion
  663.3 245.2 %reduce-scatter.13.cloned.1.call-done = f32[2048,512]{1,0:T(8,128)} async-done(((f32[2048,2048]{1,0:T(8,128)}), f32[2048,512]{1,0:T(8,128)}) %reduce-scatter.13.cloned.1.call-update) | async-done | bytes 4194320 | tf_op jit(solution)/shard_map/reduce_scatter | solution.py:240
  908.5 6.5 fusion.27
  915.1 2.1 pad_maximum_fusion.1
  920.4 250.0 %all-gather.17.cloned.1.call-done = bf16[2048,3584]{1,0:T(8,128)(2,1)} async-done(((bf16[2048,896]{1,0:T(8,128)(2,1)}), bf16[2048,3584]{1,0:T(8,128)(2,1)}) %all-gather.17.cloned.1.call-update) | async-done | bytes 14680080 | tf_op jit(solution)/shard_map/all_gather | solution.py:262
  1170.4 13.4 fusion.37
  1183.8 136.5 %all-gather.13.cloned.1.call-done = bf16[2048,2048]{1,0:T(8,128)(2,1)} async-done(((bf16[2048,512]{1,0:T(8,128)(2,1)}), bf16[2048,2048]{1,0:T(8,128)(2,1)}) %all-gather.13.cloned.1.call-update) | async-done | bytes 8388624 | tf_op jit(solution)/shard_map/all_gather | solution.py:223
  1320.3 10.5 fusion.34
  1330.8 35.5 %all-gather.11.cloned.1.call-done = bf16[2048,512]{0,1:T(8,128)(2,1)} async-done(((bf16[2048,128]{0,1:T(8,128)(2,1)}), bf16[2048,512]{0,1:T(8,128)(2,1)}) %all-gather.11.cloned.1.call-update) | async-done | bytes 2097168 | tf_op jit(solution)/shard_map/all_gather | solution.py:222
  1366.4 6.3 convolution_add_fusion
  1374.0 3.7 fusion.39
  1379.1 33.8 %reduce-scatter.15.cloned.1.call-done = f32[512,512]{1,0:T(8,128)} async-done(((f32[2048,512]{1,0:T(8,128)}), f32[512,512]{1,0:T(8,128)}) %reduce-scatter.15.cloned.1.call-update) | async-done | bytes 1048592 | tf_op jit(solution)/shard_map/reduce_scatter | solution.py:264
  1414.7 11.7 all-reduce
  1426.4 34.1 %reduce-scatter.9.cloned.1.call-done = f32[512,512]{1,0:T(8,128)} async-done(((f32[2048,512]{1,0:T(8,128)}), f32[512,512]{1,0:T(8,128)}) %reduce-scatter.9.cloned.1.call-update) | async-done | bytes 1048592 | tf_op jit(solution)/shard_map/reduce_scatter | solution.py:225
  1460.4 3.3 convert_reduce_fusion.1
  1464.6 9.9 fusion.40
  1474.5 5.9 reshape.252
  1480.4 4.8 copy.173
  1485.1 11.4 fusion.38
  1496.8 2.5 slice.150
  1503.1 5.3 copy.172
  1514.0 4.5 copy-done.4
  1520.6 4.0 copy.182
  1524.6 4.2 reshape.256
  1531.3 2.0 copy.177
  1535.7 2.4 copy.183
  1548.4 2.4 reduce_sum.141
  1551.8 120.6 %reduce-scatter.17.cloned.1.call-done = f32[1,1,12,512,256]{4,3,2,1,0:T(8,128)} async-done(((f32[1,1,24,512,256]{4,3,2,1,0:T(8,128)}), f32[1,1,12,512,256]{4,3,2,1,0:T(8,128)}) %reduce-scatter.17.cloned.1.call-update) | async-done | bytes 6291472 | tf_op jit(solution)/shard_map/reduce_scatter | solution.py:309
  1672.4 5.7 fusion.2
  1694.8 5.5 subtract_bitcast_fusion
  (203 shorter events, 87.3 us)
Async XLA Ops:
  7.2 27.7 %all-gather.15.cloned.1.call-start = ((), (), s32[]{:S(2)}) async-start(), calls=%async_computation.11 | async-start | bytes 2621440 | tf_op jit(solution)/shard_map/all_gather | solution.py:183
  7.9 51.7 %all-gather.9.cloned.1.call-start = ((), (), s32[]{:S(2)}) async-start(), calls=%async_computation.6 | async-start | bytes 2621440 | tf_op jit(solution)/shard_map/all_gather | solution.py:182
  26.5 112.8 %reduce-scatter.11.cloned.1.call-start = ((), (), s32[]{:S(2)}) async-start(), calls=%async_computation.12 | async-start | bytes 5242880 | tf_op jit(solution)/shard_map/reduce_scatter | solution.py:239
  39.8 1.6 copy-start.8
  39.9 583.9 %reduce-scatter.7.cloned.1.call-start = ((), (), s32[]{:S(2)}) async-start(), calls=%async_computation.7 | async-start | bytes 36700160 | tf_op jit(solution)/shard_map/reduce_scatter | solution.py:194
  46.1 7.7 copy-start.5
  75.8 1.6 copy-start.12
  75.8 832.7 %reduce-scatter.13.cloned.1.call-start = ((), (), s32[]{:S(2)}) async-start(), calls=%async_computation.13 | async-start | bytes 20971520 | tf_op jit(solution)/shard_map/reduce_scatter | solution.py:240
  87.1 0.9 copy-start.28
  87.1 0.9 copy-start.31
  87.1 1.0 copy-start.32
  87.1 1.1 slice-start
  87.1 1083.3 %all-gather.17.cloned.1.call-start = ((), (), s32[]{:S(2)}) async-start(), calls=%async_computation.14 | async-start | bytes 18350080 | tf_op jit(solution)/shard_map/all_gather | solution.py:262
  630.2 1.2 copy-start.7
  630.7 2.6 copy-start.25
  631.4 1.9 copy-start.23
  633.3 3.4 copy-start
  636.7 4.5 copy-start.15
  645.8 4.0 copy-start.21
  649.8 6.0 copy-start.26
  655.8 1.5 copy-start.24
  657.4 1.8 copy-start.27
  908.5 6.5 copy-start.17
  908.5 6.5 copy-start.18
  908.5 6.5 copy-start.19
  917.1 403.2 %all-gather.13.cloned.1.call-start = ((), (), s32[]{:S(2)}) async-start(), calls=%async_computation.9 | async-start | bytes 10485760 | tf_op jit(solution)/shard_map/all_gather | solution.py:223
  917.9 448.5 %all-gather.11.cloned.1.call-start = ((), (), s32[]{:S(2)}) async-start(), calls=%async_computation.8 | async-start | bytes 2621440 | tf_op jit(solution)/shard_map/all_gather | solution.py:222
  920.3 492.6 %reduce-scatter.15.cloned.1.call-start = ((), (), s32[]{:S(2)}) async-start(), calls=%async_computation.15 | async-start | bytes 5242880 | tf_op jit(solution)/shard_map/reduce_scatter | solution.py:264
  1183.8 276.6 %reduce-scatter.9.cloned.1.call-start = ((), (), s32[]{:S(2)}) async-start(), calls=%async_computation.10 | async-start | bytes 5242880 | tf_op jit(solution)/shard_map/reduce_scatter | solution.py:225
  1372.7 175.7 %all-gather.19.cloned.1.call-start = ((), (), s32[]{:S(2)}) async-start(), calls=%async_computation.17 | async-start | bytes 4325376 | tf_op jit(solution)/shard_map/all_gather | solution.py:294
  1374.0 38.9 %copy-start.11 = (bf16[512,512]{1,0:T(8,128)(2,1)S(1)}, bf16[512,512]{1,0:T(8,128)(2,1)}, u32[]{:S(2)}) copy-start(bf16[512,512]{1,0:T(8,128)(2,1)} %param.11) | copy-start | bytes 1572868
  1377.8 82.7 %copy-start.20 = (bf16[512,512]{1,0:T(8,128)(2,1)S(1)}, bf16[512,512]{1,0:T(8,128)(2,1)}, u32[]{:S(2)}) copy-start(bf16[512,512]{1,0:T(8,128)(2,1)} %param.12) | copy-start | bytes 1572868
  1379.1 85.5 %copy-start.13 = (bf16[2048,512]{1,0:T(8,128)(2,1)S(1)}, bf16[2048,512]{1,0:T(8,128)(2,1)}, u32[]{:S(2)}) copy-start(bf16[2048,512]{1,0:T(8,128)(2,1)} %all-gather.15.cloned.1.call-done) | copy-start | bytes 6291460
  1464.5 207.9 %reduce-scatter.17.cloned.1.call-start = ((), (), s32[]{:S(2)}) async-start(), calls=%async_computation.16 | async-start | bytes 18874368 | tf_op jit(solution)/shard_map/reduce_scatter | solution.py:309
  1480.3 4.8 copy-start.33
  1508.5 1.2 copy-start.16
  1508.5 2.5 copy-start.3
  1511.0 2.2 copy-start.2
  1514.0 4.5 copy-start.4
  1518.5 1.0 copy-start.14
  1520.6 8.2 copy-start.6
  1529.9 5.8 copy-start.10
  1539.9 5.5 copy-start.9
  1546.9 4.1 copy-start.29
  1546.9 4.1 copy-start.30
  1550.8 127.3 %copy-start.22 = (f32[11,2048]{1,0:T(8,128)}, f32[11,2048]{1,0:T(8,128)S(1)}, u32[]{:S(2)}) copy-start(f32[11,2048]{1,0:T(8,128)S(1)} %reduce_sum.141) | copy-start | bytes 270340
  1678.1 2.7 copy-start.1
Sparse Core Ops, SparseCore 0:
  9.5 25.2 all-gather.14
  37.0 22.5 all-gather.8
  62.5 76.7 reduce-scatter.10
  141.5 482.1 reduce-scatter.6
  625.9 282.5 reduce-scatter.12
  917.3 253.0 all-gather.16
  1172.5 147.7 all-gather.12
  1322.5 43.8 all-gather.10
  1369.5 43.3 reduce-scatter.14
  1415.8 44.5 reduce-scatter.8
  1464.7 61.6 all-gather.18
  1529.0 143.3 reduce-scatter.16
